TPU v7x, 32 devices: a whole 2x2x4 slice. The times are simulated.
32 devices in a mesh: dp: 16 (over z, x, core), tensor: 2 (over y).
Axes of the slice: x: 2, y: 2, z: 4, core: 2. Of those that a mesh axis runs over, the one named last changes fastest.
Arguments:
- x_in: bfloat16 [16, 2, 1024, 768], P(None, 'tensor', 'dp'), may hold values from -6 to 6
- cotangent: bfloat16 [16, 2, 1024, 768], P(None, 'tensor', 'dp'), may hold values from -6 to 6
- lengths: int32 [16], replicated, may hold values from 1 to 2048, 24576 in all
- dealing: int32 [16], replicated, may hold values from 0 to 15, each once
- w_qkv: float32 [768, 3, 768], P('dp', None, 'tensor'), may hold values from -0.21875 to 0.21875
- w_out: float32 [768, 768], P('dp', 'tensor'), may hold values from -1.75 to 1.75
- w_in: float32 [768, 3072], P('dp', 'tensor'), may hold values from -0.21875 to 0.21875
- w_ffo: float32 [768, 3072], P('dp', 'tensor'), may hold values from -0.109375 to 0.109375
- b_qv: float32 [2, 768], P(None, 'tensor'), may hold values from -3 to 3
- b_out: float32 [768], replicated, may hold values from -3 to 3
- b_in: float32 [3072], P('tensor'), may hold values from -3 to 3
- b_ffo: float32 [768], replicated, may hold values from -3 to 3
- ln1_gain: float32 [768], replicated, may hold values from 0.1 to 1.9
- ln1_bias: float32 [768], replicated, may hold values from -3 to 3
- ln2_gain: float32 [768], replicated, may hold values from 0.1 to 1.9
- ln2_bias: float32 [768], replicated, may hold values from -3 to 3
Outputs:
- out: bfloat16 [16, 2, 1024, 768], P(None, 'tensor', 'dp')
- grad_in: bfloat16 [16, 2, 1024, 768], P(None, 'tensor', 'dp')
- grad_w_qkv: float32 [768, 3, 768], P('dp', None, 'tensor')
- grad_w_out: float32 [768, 768], P('dp', 'tensor')
- grad_w_in: float32 [768, 3072], P('dp', 'tensor')
- grad_w_ffo: float32 [768, 3072], P('dp', 'tensor')
- grad_b_qv: float32 [2, 768], P(None, 'tensor')
- grad_b_out: float32 [768], replicated
- grad_b_in: float32 [3072], P('tensor')
- grad_b_ffo: float32 [768], replicated
- grad_ln1_gain: float32 [768], replicated
- grad_ln1_bias: float32 [768], replicated
- grad_ln2_gain: float32 [768], replicated
- grad_ln2_bias: float32 [768], replicated
Inputs may be any that keep to these rules, and one draw needn't show every extreme that they name: Slot j holds lengths[j] tokens of its sequence and padding after them; some slot is full, 2048 tokens. Sequence s goes to slot dealing[s]; every slot gets one sequence.
All inputs are finite; a program needn't handle non-finite values.
Results may differ from a plain program's by a relative error of at most 0.018.
Values may be sent and summed in bfloat16 or wider, within the bound.
A program may use at most 192 MiB of HBM per device.

v0:
```python
import jax
import jax.numpy as jnp
from jax import lax
from jax.sharding import PartitionSpec as P

HEAD_DIM = 64


def slot_owner(dealing):
    places = jnp.arange(dealing.shape[0], dtype=jnp.int32)
    matches = dealing[None, :] == places[:, None]
    return jnp.sum(jnp.where(matches, places[None, :], 0), axis=1)


def contract_last(left_side, right_side):
    return lax.dot_general(
        left_side, right_side, (((1,), (1,)), ((), ())), preferred_element_type=jnp.float32
    )


def contract_first(left_side, right_side):
    return lax.dot_general(
        left_side, right_side, (((0,), (0,)), ((), ())), preferred_element_type=jnp.float32
    )


def norm_forward(values, norm_gain, norm_shift):
    centre = jnp.mean(values, axis=-1, keepdims=True)
    centred = values - centre
    inverse = lax.rsqrt(jnp.mean(centred * centred, axis=-1, keepdims=True) + 1e-06)
    normed = centred * inverse
    return (normed * norm_gain + norm_shift, normed, inverse)


def norm_backward(upstream, normed, inverse, norm_gain):
    scaled = upstream * norm_gain
    back_rows = inverse * (
        scaled
        - jnp.mean(scaled, axis=-1, keepdims=True)
        - normed * jnp.mean(scaled * normed, axis=-1, keepdims=True)
    )
    return (back_rows, jnp.sum(upstream * normed, axis=0), jnp.sum(upstream, axis=0))


def gelu_slope(values):
    return (
        0.5 * (1.0 + lax.erf(values * 0.7071067811865476))
        + values * jnp.exp(-0.5 * values * values) * 0.3989422804014327
    )


def head_forward(query_rows, key_rows, value_rows, key_valid, block_rows, score_scale):
    outputs = []
    totals = []
    for row_start in range(0, query_rows.shape[0], block_rows):
        scores = (
            contract_last(query_rows[row_start : row_start + block_rows], key_rows) * score_scale
        )
        scores = jnp.where(key_valid[None, :], scores, -jnp.inf)
        maxima = jnp.max(scores, axis=1, keepdims=True)
        weights = jnp.exp(scores - maxima)
        summed = jnp.sum(weights, axis=1, keepdims=True)
        probs_low = (weights / summed).astype(jnp.bfloat16)
        outputs.append(jnp.dot(probs_low, value_rows, preferred_element_type=jnp.float32))
        totals.append((maxima + jnp.log(summed))[:, 0])
    return (jnp.concatenate(outputs, axis=0), jnp.concatenate(totals, axis=0))


def head_backward(
    query_rows, key_rows, value_rows, mixed_grad, log_totals, key_valid, block_rows, score_scale
):
    key_grad = jnp.zeros(key_rows.shape, jnp.float32)
    value_grad = jnp.zeros(value_rows.shape, jnp.float32)
    query_parts = []
    for row_start in range(0, query_rows.shape[0], block_rows):
        query_block = query_rows[row_start : row_start + block_rows]
        grad_block = mixed_grad[row_start : row_start + block_rows]
        scores = contract_last(query_block, key_rows) * score_scale
        scores = jnp.where(key_valid[None, :], scores, -jnp.inf)
        probs = jnp.exp(scores - log_totals[row_start : row_start + block_rows][:, None])
        prob_grad = contract_last(grad_block, value_rows)
        shared = jnp.sum(probs * prob_grad, axis=1, keepdims=True)
        score_grad = (probs * (prob_grad - shared)).astype(jnp.bfloat16)
        query_parts.append(
            jnp.dot(score_grad, key_rows, preferred_element_type=jnp.float32) * score_scale
        )
        key_grad = key_grad + contract_first(score_grad, query_block) * score_scale
        value_grad = value_grad + contract_first(probs.astype(jnp.bfloat16), grad_block)
    return (jnp.concatenate(query_parts, axis=0), key_grad, value_grad)


def per_device(
    x_in,
    cotangent,
    lengths,
    dealing,
    w_qkv,
    w_out,
    w_in,
    w_ffo,
    b_qv,
    b_out,
    b_in,
    b_ffo,
    ln1_gain,
    ln1_bias,
    ln2_gain,
    ln2_bias,
):
    owners = slot_owner(dealing)
    dealt_x, dealt_grad = (
        lax.all_to_all(
            jnp.take(x_in, owners, axis=0), "dp", split_axis=0, concat_axis=2, tiled=True
        ),
        lax.all_to_all(
            jnp.take(cotangent, owners, axis=0), "dp", split_axis=0, concat_axis=2, tiled=True
        ),
    )
    tokens_half = dealt_x[0, 0]
    output_grad = dealt_grad[0, 0].astype(jnp.float32)
    half_rows = tokens_half.shape[0]
    tensor_count = lax.axis_size("tensor")
    tensor_index = lax.axis_index("tensor")
    seq_rows = half_rows * tensor_count
    model_width = tokens_half.shape[1]
    head_width = b_qv.shape[1]
    head_count = head_width // HEAD_DIM
    ffn_width = b_in.shape[0]
    block_rows = min(512, seq_rows)
    score_scale = HEAD_DIM ** (-0.5)
    key_valid = jnp.arange(seq_rows) < lengths[lax.axis_index("dp")]
    qkv_weight, out_weight, in_weight, ffo_weight = (
        lax.all_gather(w_qkv.astype(jnp.bfloat16), "dp", axis=0, tiled=True),
        lax.all_gather(w_out.astype(jnp.bfloat16), "dp", axis=0, tiled=True),
        lax.all_gather(w_in.astype(jnp.bfloat16), "dp", axis=0, tiled=True),
        lax.all_gather(w_ffo.astype(jnp.bfloat16), "dp", axis=0, tiled=True),
    )

    def split_heads(matrix):
        return matrix.reshape(seq_rows, head_count, HEAD_DIM).transpose(1, 0, 2)

    def merge_heads(stacked):
        return stacked.transpose(1, 0, 2).reshape(seq_rows, head_width)

    tokens_full = lax.all_gather(tokens_half, "tensor", axis=0, tiled=True)
    projected = jnp.einsum(
        "ld,dce->cle", tokens_full, qkv_weight, preferred_element_type=jnp.float32
    )
    query_heads = split_heads((projected[0] + b_qv[0]).astype(jnp.bfloat16))
    key_heads = split_heads(projected[1].astype(jnp.bfloat16))
    value_heads = split_heads((projected[2] + b_qv[1]).astype(jnp.bfloat16))
    mixed_heads, log_totals = lax.map(
        lambda triple: head_forward(
            triple[0], triple[1], triple[2], key_valid, block_rows, score_scale
        ),
        (query_heads, key_heads, value_heads),
    )
    mixed_low = merge_heads(mixed_heads).astype(jnp.bfloat16)
    attn_half = lax.psum_scatter(
        contract_last(
            lax.slice_in_dim(mixed_low, 0, lax.axis_size("tensor") * half_rows, axis=0), out_weight
        ).astype(jnp.bfloat16),
        "tensor",
        scatter_dimension=0,
        tiled=True,
    ).astype(jnp.float32)
    first_norm, normed_one, inverse_one = norm_forward(
        tokens_half.astype(jnp.float32) + attn_half + b_out, ln1_gain, ln1_bias
    )
    first_full = lax.all_gather(first_norm.astype(jnp.bfloat16), "tensor", axis=0, tiled=True)
    hidden = jnp.dot(first_full, in_weight, preferred_element_type=jnp.float32) + b_in
    active = jax.nn.gelu(hidden, approximate=False).astype(jnp.bfloat16)
    ffn_half = lax.psum_scatter(
        contract_last(
            lax.slice_in_dim(active, 0, lax.axis_size("tensor") * half_rows, axis=0), ffo_weight
        ).astype(jnp.bfloat16),
        "tensor",
        scatter_dimension=0,
        tiled=True,
    ).astype(jnp.float32)
    result, normed_two, inverse_two = norm_forward(
        first_norm + ffn_half + b_ffo, ln2_gain, ln2_bias
    )
    final_grad, gain_two_grad, shift_two_grad = norm_backward(
        output_grad, normed_two, inverse_two, ln2_gain
    )
    ffo_bias_grad = jnp.sum(final_grad, axis=0)
    qkv_weight, out_weight, in_weight, ffo_weight = (
        lax.all_gather(w_qkv.astype(jnp.bfloat16), "dp", axis=0, tiled=True),
        lax.all_gather(w_out.astype(jnp.bfloat16), "dp", axis=0, tiled=True),
        lax.all_gather(w_in.astype(jnp.bfloat16), "dp", axis=0, tiled=True),
        lax.all_gather(w_ffo.astype(jnp.bfloat16), "dp", axis=0, tiled=True),
    )
    ffn_grad_full = lax.all_gather(final_grad.astype(jnp.bfloat16), "tensor", axis=0, tiled=True)
    ffo_weight_grad = contract_first(ffn_grad_full, active)
    hidden_grad = (
        jnp.dot(ffn_grad_full, ffo_weight, preferred_element_type=jnp.float32) * gelu_slope(hidden)
    ).astype(jnp.bfloat16)
    in_weight_grad = contract_first(first_full, hidden_grad)
    in_bias_grad = jnp.sum(hidden_grad.astype(jnp.float32), axis=0)
    first_grad = final_grad + lax.psum_scatter(
        contract_last(
            lax.slice_in_dim(hidden_grad, 0, lax.axis_size("tensor") * half_rows, axis=0), in_weight
        ).astype(jnp.bfloat16),
        "tensor",
        scatter_dimension=0,
        tiled=True,
    ).astype(jnp.float32)
    resid_grad, gain_one_grad, shift_one_grad = norm_backward(
        first_grad, normed_one, inverse_one, ln1_gain
    )
    out_bias_grad = jnp.sum(resid_grad, axis=0)
    attn_grad_full = lax.all_gather(resid_grad.astype(jnp.bfloat16), "tensor", axis=0, tiled=True)
    out_weight_grad = contract_first(attn_grad_full, mixed_low)
    mixed_grad = jnp.dot(attn_grad_full, out_weight, preferred_element_type=jnp.float32).astype(
        jnp.bfloat16
    )
    query_grads, key_grads, value_grads = lax.map(
        lambda bundle: head_backward(
            bundle[0],
            bundle[1],
            bundle[2],
            bundle[3],
            bundle[4],
            key_valid,
            block_rows,
            score_scale,
        ),
        (query_heads, key_heads, value_heads, split_heads(mixed_grad), log_totals),
    )
    qkv_grad = jnp.stack(
        [merge_heads(query_grads), merge_heads(key_grads), merge_heads(value_grads)]
    ).astype(jnp.bfloat16)
    qv_bias_grad = jnp.stack(
        [
            jnp.sum(qkv_grad[0].astype(jnp.float32), axis=0),
            jnp.sum(qkv_grad[2].astype(jnp.float32), axis=0),
        ]
    )
    qkv_weight_grad = jnp.einsum(
        "ld,cle->dce", tokens_full, qkv_grad, preferred_element_type=jnp.float32
    )
    rows_grad = lax.slice_in_dim(qkv_grad, 0, lax.axis_size("tensor") * half_rows, axis=1)
    input_grad = resid_grad + lax.psum_scatter(
        jnp.einsum("cle,dce->ld", rows_grad, qkv_weight, preferred_element_type=jnp.float32).astype(
            jnp.bfloat16
        ),
        "tensor",
        scatter_dimension=0,
        tiled=True,
    ).astype(jnp.float32)
    qkv_sum, out_sum, in_sum, ffo_sum = (
        lax.psum_scatter(qkv_weight_grad, "dp", scatter_dimension=0, tiled=True),
        lax.psum_scatter(out_weight_grad, "dp", scatter_dimension=0, tiled=True),
        lax.psum_scatter(in_weight_grad, "dp", scatter_dimension=0, tiled=True),
        lax.psum_scatter(ffo_weight_grad, "dp", scatter_dimension=0, tiled=True),
    )
    norm_terms = jnp.stack(
        [out_bias_grad, ffo_bias_grad, gain_one_grad, shift_one_grad, gain_two_grad, shift_two_grad]
    )
    qv_padded = lax.dynamic_update_slice_in_dim(
        jnp.zeros((2, model_width), jnp.float32), qv_bias_grad, tensor_index * head_width, 1
    )
    in_padded = lax.dynamic_update_slice_in_dim(
        jnp.zeros((ffn_width * tensor_count,), jnp.float32),
        in_bias_grad,
        tensor_index * ffn_width,
        0,
    )
    norm_sums, qv_sums, in_sums = lax.psum((norm_terms, qv_padded, in_padded), ("dp", "tensor"))
    qv_share = lax.dynamic_slice_in_dim(qv_sums, tensor_index * head_width, head_width, 1)
    in_share = lax.dynamic_slice_in_dim(in_sums, tensor_index * ffn_width, ffn_width, 0)
    back_out, back_grad = (
        lax.all_to_all(
            result.astype(jnp.bfloat16)[None, None], "dp", split_axis=2, concat_axis=0, tiled=True
        ),
        lax.all_to_all(
            input_grad.astype(jnp.bfloat16)[None, None],
            "dp",
            split_axis=2,
            concat_axis=0,
            tiled=True,
        ),
    )
    return (
        jnp.take(back_out, dealing, axis=0),
        jnp.take(back_grad, dealing, axis=0),
        qkv_sum,
        out_sum,
        in_sum,
        ffo_sum,
        qv_share,
        norm_sums[0],
        in_share,
        norm_sums[1],
        norm_sums[2],
        norm_sums[3],
        norm_sums[4],
        norm_sums[5],
    )


def solution(mesh):
    return jax.shard_map(
        per_device,
        mesh=mesh,
        in_specs=(
            P(None, "tensor", "dp", None),
            P(None, "tensor", "dp", None),
            P(),
            P(),
            P("dp", None, "tensor"),
            P("dp", "tensor"),
            P("dp", "tensor"),
            P("dp", "tensor"),
            P(None, "tensor"),
            P(),
            P("tensor"),
            P(),
            P(),
            P(),
            P(),
            P(),
        ),
        out_specs=(
            P(None, "tensor", "dp", None),
            P(None, "tensor", "dp", None),
            P("dp", None, "tensor"),
            P("dp", "tensor"),
            P("dp", "tensor"),
            P("dp", "tensor"),
            P(None, "tensor"),
            P(),
            P("tensor"),
            P(),
            P(),
            P(),
            P(),
            P(),
        ),
        check_vma=False,
    )
```

profile of v0, /device:TPU:0, one launch (start us, length us, event | category | flops | bytes accessed | tf_op | source)
XLA Modules:
  0.0 1286.9 jit_solution(3330152919851395239)
XLA Ops:
  16.4 53.0 %all_to_all.42 = bf16[16,1,64,768]{3,2,1,0:T(8,128)(2,1)} all-to-all(bf16[16,1,64,768]{3,2,1,0:T(8,128)(2,1)S(1)} %get-tuple-element.272), channel_id=1, replica_groups=mesh['dp'=16,'tensor'=2] {'dp'}, dimensions={0} | all-to-all | bytes 3145728 | tf_op jit(solution)/shard_map/all_to_all | solution.py:112
  70.2 23.6 %all_gather.30 = bf16[768,384]{1,0:T(8,128)(2,1)} all-gather(bf16[48,384]{1,0:T(8,128)(2,1)S(1)} %convert_element_type.160), channel_id=1, replica_groups=mesh['dp'=16,'tensor'=2] {'dp'}, dimensions={0}, use_global_device_ids=true | all-gather | bytes 626688 | tf_op jit(solution)/shard_map/all_gather | solution.py:134
  93.8 20.8 %all-gather.8.cloned.1.call-done = bf16[2048,768]{1,0:T(8,128)(2,1)} async-done(((bf16[1024,768]{1,0:T(8,128)(2,1)}), bf16[2048,768]{1,0:T(8,128)(2,1)}) %all-gather.8.cloned.1.call-update) | async-done | bytes 3145744 | tf_op jit(solution)/shard_map/all_gather | solution.py:145
  114.7 6.5 convolution_bitcast_fusion
  148.9 117.0 %while.28 = (s32[]{:T(128)}, bf16[6,2048,64]{1,2,0:T(8,128)(2,1)}, f32[6,2048]{1,0:T(8,128)}, bf16[6,2048,64]{2,1,0:T(8,128)(2,1)}, bf16[6,2048,64]{2,1,0:T(8,12...) while((s32[]{:T(128)}, bf16[6,2048,64]{1,2,0:T(8,128)(2,1)}, ...), condition=%wide.region_10.12_spmd.clone, body=%wide.region_1.11_spmd.clone.sunk | while | flops 1125128192 | bytes 70637272 | solution.py:152
  273.8 41.9 %reduce-scatter.9.cloned.1.call-done = bf16[1024,768]{1,0:T(8,128)(2,1)} async-done(((bf16[2048,768]{1,0:T(8,128)(2,1)}), bf16[1024,768]{1,0:T(8,128)(2,1)}) %reduce-scatter.9.cloned.1.call-update) | async-done | bytes 1572880 | tf_op jit(solution)/shard_map/reduce_scatter | solution.py:159
  321.6 39.1 %all-gather.14.cloned.1.call-done = bf16[768,1536]{1,0:T(8,128)(2,1)} async-done(((bf16[48,1536]{1,0:T(8,128)(2,1)}), bf16[768,1536]{1,0:T(8,128)(2,1)}) %all-gather.14.cloned.1.call-update) | async-done | bytes 2359312 | tf_op jit(solution)/shard_map/all_gather | solution.py:135
  360.7 45.1 %all-gather.12.cloned.1.call-done = bf16[2048,768]{1,0:T(8,128)(2,1)} async-done(((bf16[1024,768]{1,0:T(8,128)(2,1)}), bf16[2048,768]{1,0:T(8,128)(2,1)}) %all-gather.12.cloned.1.call-update) | async-done | bytes 3145744 | tf_op jit(solution)/shard_map/all_gather | solution.py:170
  405.8 34.6 %fusion.115 = (bf16[2048,1536]{1,0:T(8,128)(2,1)}, f32[2048,1536]{1,0:T(8,128)}) fusion(f32[1536]{0:T(1024)S(1)} %copy-done.49, bf16[2048,768]{1,0:T(8,128)(2,1)} %all-gather.12.cloned.1.call-done, bf16[768,1536]{1,0:T(8,128)(2,1)} %all-gather.14.cloned.1.call-done), kind=kOutput, calls=%fused_computation.175 | convolution fusion | flops 5039456256 | bytes 24385536 | tf_op jit(solution)/shard_map/dot_general | solution.py:171
  440.4 10.5 all-gather.16.cloned.1.call-done
  450.8 9.0 convolution_convert_fusion.2
  460.0 40.0 %all_to_all.43 = bf16[16,1,64,768]{3,2,1,0:T(8,128)(2,1)S(1)} all-to-all(bf16[16,1,64,768]{3,2,1,0:T(8,128)(2,1)} %get-tuple-element.271), channel_id=1, replica_groups=mesh['dp'=16,'tensor'=2] {'dp'}, dimensions={0} | all-to-all | bytes 3145728 | tf_op jit(solution)/shard_map/all_to_all | solution.py:115
  512.0 45.3 %all-gather.18.cloned.1.call-done = bf16[2048,768]{1,0:T(8,128)(2,1)} async-done(((bf16[1024,768]{1,0:T(8,128)(2,1)}), bf16[2048,768]{1,0:T(8,128)(2,1)}) %all-gather.18.cloned.1.call-update) | async-done | bytes 3145744 | tf_op jit(solution)/shard_map/all_gather | solution.py:194
  557.3 12.4 convert_reduce_fusion
  572.3 6.4 convolution_convert_fusion.1
  578.8 43.5 %reduce-scatter.13.cloned.1.call-done = bf16[1024,768]{1,0:T(8,128)(2,1)} async-done(((bf16[2048,768]{1,0:T(8,128)(2,1)}), bf16[1024,768]{1,0:T(8,128)(2,1)}) %reduce-scatter.13.cloned.1.call-update) | async-done | bytes 1572880 | tf_op jit(solution)/shard_map/reduce_scatter | solution.py:201
  632.4 45.0 %all-gather.20.cloned.1.call-done = bf16[2048,768]{1,0:T(8,128)(2,1)} async-done(((bf16[1024,768]{1,0:T(8,128)(2,1)}), bf16[2048,768]{1,0:T(8,128)(2,1)}) %all-gather.20.cloned.1.call-update) | async-done | bytes 3145744 | tf_op jit(solution)/shard_map/all_gather | solution.py:213
  687.6 217.3 %while.29 = (s32[]{:T(128)}, bf16[6,2048,64]{1,2,0:T(8,128)(2,1)}, bf16[6,2048,64]{1,2,0:T(8,128)(2,1)}, bf16[6,2048,64]{1,2,0:T(8,128)(2,1)}, bf16[6,2048,64]{2...) while((s32[]{:T(128)}, bf16[6,2048,64]{1,2,0:T(8,128)(2,1)}, ...), condition=%wide.region_27.29_spmd.clone, body=%wide.region_22.28_spmd.clone.sunk | while | flops 2724331520 | bytes 161284432 | solution.py:218
  910.9 8.5 bitcast_convert_fusion
  921.3 9.6 fusion.157
  932.8 9.5 fusion.156
  952.8 11.5 reduce.24
  974.7 8.7 fusion.138
  989.8 11.5 reduce.23
  1005.9 9.2 all-to-all-done.1
  1015.1 19.2 %all-to-all-start.3 = ((bf16[16,2,24576]{2,1,0:T(2,128)(2,1)}), bf16[16,2,24576]{2,1,0:T(2,128)(2,1)}, u32[]{:S(2)}, u32[]{:S(2)}) async-start(bf16[16,2,24576]{2,1,0:T(2,128)(2,1)} %reshape.277), calls=%async_computation.7 | async-start | bytes 3145728 | tf_op jit(solution)/shard_map/all_to_all | solution.py:277
  1034.4 10.1 reshape.276
  1052.3 48.6 %all-reduce = (f32[2,768]{1,0:T(2,128)S(1)}, f32[6,768]{1,0:T(8,128)S(1)}, f32[3072]{0:T(1024)S(1)}) all-reduce(f32[2,768]{1,0:T(2,128)S(1)} %maximum_dynamic-update-slice_fusion, f32[6,768]{1,0:T(8,128)S(1)} %stack.44, f32[3072]{0:T(1024)S(1)} %dynamic_update_slice.24), channel_id=1, replica_groups=mesh['dp'=16,'tensor'=2] {'dp','tensor'}, use_global_device_ids=true, to_apply=%region_35.37 | all-reduce | flops 9216 | bytes 73728 | tf_op jit(solution)/shard_map/psum | solution.py:270
  1102.8 8.1 reshape.278
  1119.2 28.1 %reduce-scatter.21.cloned.1.call-done = f32[48,1536]{1,0:T(8,128)} async-done(((f32[768,1536]{1,0:T(8,128)}), f32[48,1536]{1,0:T(8,128)}) %reduce-scatter.21.cloned.1.call-update) | async-done | bytes 294928 | tf_op jit(solution)/shard_map/reduce_scatter | solution.py:255
  1147.3 61.5 %reduce-scatter.19.cloned.1.call-done = f32[48,384]{1,0:T(8,128)} async-done(((f32[768,384]{1,0:T(8,128)}), f32[48,384]{1,0:T(8,128)}) %reduce-scatter.19.cloned.1.call-update) | async-done | bytes 73744 | tf_op jit(solution)/shard_map/reduce_scatter | solution.py:254
  1208.7 71.4 %reduce-scatter.17.cloned.1.call-done = f32[48,3,384]{2,0,1:T(8,128)} async-done(((f32[768,3,384]{2,0,1:T(8,128)}), f32[48,3,384]{2,0,1:T(8,128)}) %reduce-scatter.17.cloned.1.call-update) | async-done | bytes 221200 | tf_op jit(solution)/shard_map/reduce_scatter | solution.py:253
  (516 shorter events, 477.7 us)
Async XLA Ops:
  7.2 86.6 %all-gather.10.cloned.1.call-start = ((), (), s32[]{:S(2)}) async-start(), calls=%async_computation.13 | async-start | bytes 1880064 | tf_op jit(solution)/shard_map/all_gather | solution.py:133
  9.0 105.7 %all-gather.8.cloned.1.call-start = ((), (), s32[]{:S(2)}) async-start(), calls=%async_computation.12 | async-start | bytes 4718592 | tf_op jit(solution)/shard_map/all_gather | solution.py:145
  16.4 53.1 %copy-start.43 = (f32[2,384]{1,0:T(2,128)S(1)}, f32[2,384]{1,0:T(2,128)}, u32[]{:S(2)}) copy-start(f32[2,384]{1,0:T(2,128)} %param.30) | copy-start | bytes 9220
  16.4 53.3 %copy-start.30 = (f32[48,384]{1,0:T(8,128)S(1)}, f32[48,384]{1,0:T(8,128)}, u32[]{:S(2)}) copy-start(f32[48,384]{1,0:T(8,128)} %param.27) | copy-start | bytes 221188
  16.4 53.3 %copy-start.50 = (s32[16]{0:T(128)S(1)}, s32[16]{0:T(128)}, u32[]{:S(2)}) copy-start(s32[16]{0:T(128)} %param.24) | copy-start | bytes 196
  69.4 246.3 %reduce-scatter.9.cloned.1.call-start = ((), (), s32[]{:S(2)}) async-start(), calls=%async_computation.14 | async-start | bytes 4718592 | tf_op jit(solution)/shard_map/reduce_scatter | solution.py:159
  272.0 43.6 %copy-start.29 = (f32[768]{0:T(1024)S(1)}, f32[768]{0:T(1024)}, u32[]{:S(2)}) copy-start(f32[768]{0:T(1024)} %param.31) | copy-start | bytes 9220
  272.0 43.6 %copy-start.4 = (bf16[16,1,64,768]{3,2,1,0:T(8,128)(2,1)S(1)}, bf16[16,1,64,768]{3,2,1,0:T(8,128)(2,1)}, u32[]{:S(2)}) copy-start(bf16[16,1,64,768]{3,2,1,0:T(8,128)(2,1)} %all_to_all.42) | copy-start | bytes 4718596
  272.1 88.6 %all-gather.14.cloned.1.call-start = ((), (), s32[]{:S(2)}) async-start(), calls=%async_computation.16 | async-start | bytes 2506752 | tf_op jit(solution)/shard_map/all_gather | solution.py:135
  273.7 45.0 %copy-start.31 = (f32[768]{0:T(1024)S(1)}, f32[768]{0:T(1024)}, u32[]{:S(2)}) copy-start(f32[768]{0:T(1024)} %param.34) | copy-start | bytes 9220
  273.7 45.0 %copy-start.38 = (f32[768]{0:T(1024)S(1)}, f32[768]{0:T(1024)}, u32[]{:S(2)}) copy-start(f32[768]{0:T(1024)} %param.35) | copy-start | bytes 9220
  273.7 132.0 %all-gather.12.cloned.1.call-start = ((), (), s32[]{:S(2)}) async-start(), calls=%async_computation.15 | async-start | bytes 4718592 | tf_op jit(solution)/shard_map/all_gather | solution.py:170
  318.7 87.1 %copy-start.49 = (f32[1536]{0:T(1024)S(1)}, f32[1536]{0:T(1024)}, u32[]{:S(2)}) copy-start(f32[1536]{0:T(1024)} %param.32) | copy-start | bytes 18436
  320.8 130.0 %all-gather.16.cloned.1.call-start = ((), (), s32[]{:S(2)}) async-start(), calls=%async_computation.17 | async-start | bytes 2506752 | tf_op jit(solution)/shard_map/all_gather | solution.py:136
  321.6 180.9 %reduce-scatter.11.cloned.1.call-start = ((), (), s32[]{:S(2)}) async-start(), calls=%async_computation.18 | async-start | bytes 4718592 | tf_op jit(solution)/shard_map/reduce_scatter | solution.py:173
  459.9 41.2 %copy-start.32 = (f32[768]{0:T(1024)S(1)}, f32[768]{0:T(1024)}, u32[]{:S(2)}) copy-start(f32[768]{0:T(1024)} %param.36) | copy-start | bytes 9220
  459.9 42.6 %copy-start.41 = (f32[768]{0:T(1024)S(1)}, f32[768]{0:T(1024)}, u32[]{:S(2)}) copy-start(f32[768]{0:T(1024)} %param.33) | copy-start | bytes 9220
  459.9 97.4 %all-gather.18.cloned.1.call-start = ((), (), s32[]{:S(2)}) async-start(), calls=%async_computation.19 | async-start | bytes 4718592 | tf_op jit(solution)/shard_map/all_gather | solution.py:194
  512.0 110.4 %reduce-scatter.13.cloned.1.call-start = ((), (), s32[]{:S(2)}) async-start(), calls=%async_computation.20 | async-start | bytes 4718592 | tf_op jit(solution)/shard_map/reduce_scatter | solution.py:201
  578.8 98.7 %all-gather.20.cloned.1.call-start = ((), (), s32[]{:S(2)}) async-start(), calls=%async_computation.21 | async-start | bytes 4718592 | tf_op jit(solution)/shard_map/all_gather | solution.py:213
  631.1 46.4 %copy-start.26 = (bf16[768,384]{1,0:T(8,128)(2,1)S(1)}, bf16[768,384]{1,0:T(8,128)(2,1)}, u32[]{:S(2)}) copy-start(bf16[768,384]{1,0:T(8,128)(2,1)} %all_gather.30) | copy-start | bytes 1769476
  632.4 351.1 %reduce-scatter.15.cloned.1.call-start = ((), (), s32[]{:S(2)}) async-start(), calls=%async_computation.22 | async-start | bytes 4718592 | tf_op jit(solution)/shard_map/reduce_scatter | solution.py:244
  919.5 199.7 %reduce-scatter.23.cloned.1.call-start = ((), (), s32[]{:S(2)}) async-start(), calls=%async_computation.26 | async-start | bytes 5013504 | tf_op jit(solution)/shard_map/reduce_scatter | solution.py:256
  930.9 216.3 %reduce-scatter.21.cloned.1.call-start = ((), (), s32[]{:S(2)}) async-start(), calls=%async_computation.25 | async-start | bytes 5013504 | tf_op jit(solution)/shard_map/reduce_scatter | solution.py:255
  942.3 266.4 %reduce-scatter.19.cloned.1.call-start = ((), (), s32[]{:S(2)}) async-start(), calls=%async_computation.24 | async-start | bytes 1253376 | tf_op jit(solution)/shard_map/reduce_scatter | solution.py:254
  969.0 46.1 %all-to-all-start.1 = ((bf16[16,2,24576]{2,1,0:T(2,128)(2,1)}), bf16[16,2,24576]{2,1,0:T(2,128)(2,1)}, u32[]{:S(2)}, u32[]{:S(2)}) async-start(bf16[16,2,24576]{2,1,0:T(2,128)(2,1)} %reshape.275), calls=%async_computation.3 | async-start | bytes 3145728 | tf_op jit(solution)/shard_map/all_to_all | solution.py:274
  974.7 305.5 %reduce-scatter.17.cloned.1.call-start = ((), (), s32[]{:S(2)}) async-start(), calls=%async_computation.23 | async-start | bytes 3760128 | tf_op jit(solution)/shard_map/reduce_scatter | solution.py:253
  1001.3 33.0 %copy-start.45 = (s32[16]{0:T(128)S(1)}, s32[16]{0:T(128)}, u32[]{:S(2)}) copy-start(s32[16]{0:T(128)} %get-tuple-element.277) | copy-start | bytes 196
  1001.3 33.0 %copy-start.36 = (f32[768]{0:T(1024)S(1)}, f32[768]{0:T(1024)}, u32[]{:S(2)}) copy-start(f32[768]{0:T(1024)} %get-tuple-element.194) | copy-start | bytes 9220
  1001.3 33.1 %copy-start.39 = (f32[768]{0:T(1024)S(1)}, f32[768]{0:T(1024)}, u32[]{:S(2)}) copy-start(f32[768]{0:T(1024)} %get-tuple-element.189) | copy-start | bytes 9220
  1015.1 87.7 %all-to-all-start.3 = ((bf16[16,2,24576]{2,1,0:T(2,128)(2,1)}), bf16[16,2,24576]{2,1,0:T(2,128)(2,1)}, u32[]{:S(2)}, u32[]{:S(2)}) async-start(bf16[16,2,24576]{2,1,0:T(2,128)(2,1)} %reshape.277), calls=%async_computation.7 | async-start | bytes 3145728 | tf_op jit(solution)/shard_map/all_to_all | solution.py:277
  1115.7 164.5 %copy-start.1 = (bf16[16,1,64,768]{3,2,1,0:T(8,128)(2,1)S(1)}, bf16[16,1,64,768]{3,2,1,0:T(8,128)(2,1)}, u32[]{:S(2)}) copy-start(bf16[16,1,64,768]{3,2,1,0:T(8,128)(2,1)} %param.23) | copy-start | bytes 4718596
  (57 other events, 215.0 us)
Sparse Core Ops, SparseCore 0:
  10.9 53.5 all-gather.9
  69.5 45.1 all-gather.7
  272.2 43.4 reduce-scatter.8
  318.4 42.2 all-gather.13
  362.1 43.6 all-gather.11
  408.5 42.2 all-gather.15
  460.0 42.1 reduce-scatter.10
  512.1 45.1 all-gather.17
  578.9 43.4 reduce-scatter.12
  632.5 44.8 all-gather.19
  919.6 43.4 reduce-scatter.14
  967.3 94.5 reduce-scatter.22
  1066.4 80.8 reduce-scatter.20
  1151.3 57.3 reduce-scatter.18
  1213.0 67.1 reduce-scatter.16
where the time goes:
time: 1300 us; the launch traced here: 1290 us
  waiting for transfers between devices  462 us (36%)
  matrix products  388 us (30%)
  blocking collectives  165 us (13%)
  local copies, waits for them, and re-layouts  116 us (9%)
  other arithmetic  113 us (9%)
  starting transfers between devices  25.9 us (2%)
  between operations  14.7 us (1%)
    dot_general x75, matrix products, contract_last(): lax.dot_general(left_side, right_side, (((1,), (1,)), ((), ())), preferre...  168 us
    dot_general x51, matrix products, contract_first(): lax.dot_general(left_side, right_side, (((0,), (0,)), ((), ())), preferre...  97.7 us
    reduce_scatter x1, waiting for transfers between devices, per_device(): lax.psum_scatter(qkv_weight_grad, 'dp', scatter_dimension=0, tiled=True)  71.4 us
    reduce_scatter x1, waiting for transfers between devices, per_device(): lax.psum_scatter(out_weight_grad, 'dp', scatter_dimension=0, tiled=True)  61.5 us
    all_to_all x1, blocking collectives, per_device(): lax.all_to_all(jnp.take(x_in, owners, axis=0), 'dp', split_axis=0, concat...  53 us
    psum x1, blocking collectives, per_device(): lax.psum((norm_terms, qv_padded, in_padded), ('dp', 'tensor'))  48.6 us
    unnamed x103, local copies, waits for them, and re-layouts  46.6 us
    all_gather x1, waiting for transfers between devices, per_device(): lax.all_gather(final_grad.astype(jnp.bfloat16), 'tensor', axis=0, tiled=T...  45.3 us
  transfers between devices with their start and end apart: 17, of which 12 were waited for; matrix products, arithmetic and copies ran while one was open for 12% of the time, Pallas kernels for 0%

commit v1 on v0

--- a/solution.py
+++ b/solution.py
@@ -4,6 +4,29 @@
 from jax.sharding import PartitionSpec as P
 
 HEAD_DIM = 64
+
+
+def cut_along(array, dim, peers):
+    shape = array.shape
+    tiles = array.reshape(*shape[:dim], peers, shape[dim] // peers, *shape[dim + 1 :])
+    return jnp.moveaxis(tiles, dim, 0)
+
+
+def laid_out(parts, dim):
+    parts = jnp.moveaxis(parts, 0, dim)
+    dims = parts.shape
+    return parts.reshape(*dims[:dim], dims[dim] * dims[dim + 1], *dims[dim + 2 :])
+
+
+def exchange_directly(shard, axis, split_dim, concat_dim):
+    count, mine = (lax.axis_size(axis), lax.axis_index(axis))
+    parts = cut_along(shard, split_dim, count)
+    outs = [parts[mine]]
+    for step in range(1, count):
+        sent = parts[(mine + step) % count]
+        outs.append(lax.ppermute(sent, axis, [(i, (i + step) % count) for i in range(count)]))
+    parts = jnp.stack(outs)[(mine - jnp.arange(count)) % count]
+    return laid_out(parts, concat_dim)
 
 
 def slot_owner(dealing):
@@ -109,9 +132,7 @@
 ):
     owners = slot_owner(dealing)
     dealt_x, dealt_grad = (
-        lax.all_to_all(
-            jnp.take(x_in, owners, axis=0), "dp", split_axis=0, concat_axis=2, tiled=True
-        ),
+        exchange_directly(jnp.take(x_in, owners, axis=0), "dp", 0, 2),
         lax.all_to_all(
             jnp.take(cotangent, owners, axis=0), "dp", split_axis=0, concat_axis=2, tiled=True
         ),

time: 1300 us -> 1370 us (1.054)
  waiting for transfers between devices: 462 us -> 561 us
  blocking collectives: 165 us -> 115 us
    ppermute x0 -> x15, waiting for transfers between devices: none -> 57.3 us  [exchange_directly(): lax.ppermute(sent, axis, [(i, (i + step) % count) for i in range(count)])]
    all_to_all x1 -> x0, blocking collectives: 53 us -> none  [per_device(): lax.all_to_all(jnp.take(x_in, owners, axis=0), 'dp', split_axis=0, concat...]
    all_gather x1, waiting for transfers between devices: 0.01 us -> 43.4 us  [per_device(): lax.all_gather(w_qkv.astype(jnp.bfloat16), 'dp', axis=0, tiled=True)]
    unnamed x103 -> x124, local copies, waits for them, and re-layouts: 46.6 us -> 50.1 us
  transfers between devices with their start and end apart: 17 -> 32, of which waited for: 12 -> 24; matrix products, arithmetic and copies ran while one was open for 12% -> 12% of each run, Pallas kernels for 0% -> 0%
where the time goes in v1:
time: 1370 us; the launch traced here: 1350 us
  waiting for transfers between devices  561 us (41%)
  matrix products  388 us (28%)
  local copies, waits for them, and re-layouts  123 us (9%)
  blocking collectives  115 us (8%)
  other arithmetic  112 us (8%)
  starting transfers between devices  37.9 us (3%)
  between operations  15 us (1%)
    dot_general x75, matrix products, contract_last(): lax.dot_general(left_side, right_side, (((1,), (1,)), ((), ())), preferre...  168 us
    dot_general x51, matrix products, contract_first(): lax.dot_general(left_side, right_side, (((0,), (0,)), ((), ())), preferre...  97.7 us
    reduce_scatter x1, waiting for transfers between devices, per_device(): lax.psum_scatter(qkv_weight_grad, 'dp', scatter_dimension=0, tiled=True)  71.6 us
    reduce_scatter x1, waiting for transfers between devices, per_device(): lax.psum_scatter(out_weight_grad, 'dp', scatter_dimension=0, tiled=True)  61.4 us
    ppermute x15, waiting for transfers between devices, exchange_directly(): lax.ppermute(sent, axis, [(i, (i + step) % count) for i in range(count)])  57.3 us
    unnamed x124, local copies, waits for them, and re-layouts  50.1 us
    psum x1, blocking collectives, per_device(): lax.psum((norm_terms, qv_padded, in_padded), ('dp', 'tensor'))  48.6 us
    all_gather x1, waiting for transfers between devices, per_device(): lax.all_gather(first_norm.astype(jnp.bfloat16), 'tensor', axis=0, tiled=T...  45.6 us
  transfers between devices with their start and end apart: 32, of which 24 were waited for; matrix products, arithmetic and copies ran while one was open for 12% of the time, Pallas kernels for 0%

profile of v1, /device:TPU:0, one launch (start us, length us, event | category | flops | bytes accessed | tf_op | source)
XLA Modules:
  0.0 1354.6 jit_solution(13086367192912462280)
XLA Ops:
  85.9 27.4 %all_gather.30 = bf16[768,384]{1,0:T(8,128)(2,1)} all-gather(bf16[48,384]{1,0:T(8,128)(2,1)S(1)} %convert_element_type.160), channel_id=1, replica_groups=mesh['dp'=16,'tensor'=2] {'dp'}, dimensions={0}, use_global_device_ids=true | all-gather | bytes 626688 | tf_op jit(solution)/shard_map/all_gather | solution.py:155
  113.2 20.3 %all-gather.8.cloned.1.call-done = bf16[2048,768]{1,0:T(8,128)(2,1)} async-done(((bf16[1024,768]{1,0:T(8,128)(2,1)}), bf16[2048,768]{1,0:T(8,128)(2,1)}) %all-gather.8.cloned.1.call-update) | async-done | bytes 3145744 | tf_op jit(solution)/shard_map/all_gather | solution.py:166
  133.6 43.4 %all-gather.10.cloned.1.call-done = bf16[768,3,384]{2,0,1:T(8,128)(2,1)} async-done(((bf16[48,3,384]{2,0,1:T(8,128)(2,1)}), bf16[768,3,384]{2,0,1:T(8,128)(2,1)}) %all-gather.10.cloned.1.call-update) | async-done | bytes 1769488 | tf_op jit(solution)/shard_map/all_gather | solution.py:154
  176.9 6.5 convolution_bitcast_fusion
  202.4 8.7 fusion.129
  212.4 117.0 %while.28 = (s32[]{:T(128)}, bf16[6,2048,64]{1,2,0:T(8,128)(2,1)}, f32[6,2048]{1,0:T(8,128)}, bf16[6,2048,64]{2,1,0:T(8,128)(2,1)}, bf16[6,2048,64]{2,1,0:T(8,12...) while((s32[]{:T(128)}, bf16[6,2048,64]{1,2,0:T(8,128)(2,1)}, ...), condition=%wide.region_10.12_spmd.clone, body=%wide.region_1.11_spmd.clone.sunk | while | flops 1125128192 | bytes 70637272 | solution.py:173
  337.3 40.6 %reduce-scatter.9.cloned.1.call-done = bf16[1024,768]{1,0:T(8,128)(2,1)} async-done(((bf16[2048,768]{1,0:T(8,128)(2,1)}), bf16[1024,768]{1,0:T(8,128)(2,1)}) %reduce-scatter.9.cloned.1.call-update) | async-done | bytes 1572880 | tf_op jit(solution)/shard_map/reduce_scatter | solution.py:180
  383.8 39.1 %all-gather.14.cloned.1.call-done = bf16[768,1536]{1,0:T(8,128)(2,1)} async-done(((bf16[48,1536]{1,0:T(8,128)(2,1)}), bf16[768,1536]{1,0:T(8,128)(2,1)}) %all-gather.14.cloned.1.call-update) | async-done | bytes 2359312 | tf_op jit(solution)/shard_map/all_gather | solution.py:156
  422.9 45.6 %all-gather.12.cloned.1.call-done = bf16[2048,768]{1,0:T(8,128)(2,1)} async-done(((bf16[1024,768]{1,0:T(8,128)(2,1)}), bf16[2048,768]{1,0:T(8,128)(2,1)}) %all-gather.12.cloned.1.call-update) | async-done | bytes 3145744 | tf_op jit(solution)/shard_map/all_gather | solution.py:191
  468.5 34.6 %fusion.115 = (bf16[2048,1536]{1,0:T(8,128)(2,1)}, f32[2048,1536]{1,0:T(8,128)}) fusion(f32[1536]{0:T(1024)S(1)} %copy-done.51, bf16[2048,768]{1,0:T(8,128)(2,1)} %all-gather.12.cloned.1.call-done, bf16[768,1536]{1,0:T(8,128)(2,1)} %all-gather.14.cloned.1.call-done), kind=kOutput, calls=%fused_computation.176 | convolution fusion | flops 5039456256 | bytes 24385536 | tf_op jit(solution)/shard_map/dot_general | solution.py:192
  503.1 10.4 all-gather.16.cloned.1.call-done
  513.6 9.0 convolution_convert_fusion.2
  527.7 39.5 %all_to_all.33 = bf16[16,1,64,768]{3,2,1,0:T(8,128)(2,1)S(1)} all-to-all(bf16[16,1,64,768]{3,2,1,0:T(8,128)(2,1)S(1)} %bitcast_select_fusion.1), channel_id=1, replica_groups=mesh['dp'=16,'tensor'=2] {'dp'}, dimensions={0} | all-to-all | bytes 3145728 | tf_op jit(solution)/shard_map/all_to_all | solution.py:136
  579.3 45.4 %all-gather.18.cloned.1.call-done = bf16[2048,768]{1,0:T(8,128)(2,1)} async-done(((bf16[1024,768]{1,0:T(8,128)(2,1)}), bf16[2048,768]{1,0:T(8,128)(2,1)}) %all-gather.18.cloned.1.call-update) | async-done | bytes 3145744 | tf_op jit(solution)/shard_map/all_gather | solution.py:215
  624.7 12.4 convert_reduce_fusion
  646.3 43.5 %reduce-scatter.13.cloned.1.call-done = bf16[1024,768]{1,0:T(8,128)(2,1)} async-done(((bf16[2048,768]{1,0:T(8,128)(2,1)}), bf16[1024,768]{1,0:T(8,128)(2,1)}) %reduce-scatter.13.cloned.1.call-update) | async-done | bytes 1572880 | tf_op jit(solution)/shard_map/reduce_scatter | solution.py:222
  699.9 45.0 %all-gather.20.cloned.1.call-done = bf16[2048,768]{1,0:T(8,128)(2,1)} async-done(((bf16[1024,768]{1,0:T(8,128)(2,1)}), bf16[2048,768]{1,0:T(8,128)(2,1)}) %all-gather.20.cloned.1.call-update) | async-done | bytes 3145744 | tf_op jit(solution)/shard_map/all_gather | solution.py:234
  755.1 217.3 %while.29 = (s32[]{:T(128)}, bf16[6,2048,64]{1,2,0:T(8,128)(2,1)}, bf16[6,2048,64]{1,2,0:T(8,128)(2,1)}, bf16[6,2048,64]{1,2,0:T(8,128)(2,1)}, bf16[6,2048,64]{2...) while((s32[]{:T(128)}, bf16[6,2048,64]{1,2,0:T(8,128)(2,1)}, ...), condition=%wide.region_27.29_spmd.clone, body=%wide.region_22.28_spmd.clone.sunk | while | flops 2724331520 | bytes 161284432 | solution.py:239
  978.3 8.5 bitcast_convert_fusion
  988.8 9.6 fusion.159
  1000.2 9.5 fusion.158
  1020.3 11.6 reduce.24
  1042.3 8.7 fusion.138
  1057.3 11.6 reduce.23
  1073.5 9.1 all-to-all-done
  1082.6 19.2 %all-to-all-start.2 = ((bf16[16,2,24576]{2,1,0:T(2,128)(2,1)}), bf16[16,2,24576]{2,1,0:T(2,128)(2,1)}, u32[]{:S(2)}, u32[]{:S(2)}) async-start(bf16[16,2,24576]{2,1,0:T(2,128)(2,1)} %reshape.369), calls=%async_computation.6 | async-start | bytes 3145728 | tf_op jit(solution)/shard_map/all_to_all | solution.py:298
  1102.0 10.1 reshape.368
  1119.9 48.6 %all-reduce = (f32[2,768]{1,0:T(2,128)S(1)}, f32[6,768]{1,0:T(8,128)S(1)}, f32[3072]{0:T(1024)S(1)}) all-reduce(f32[2,768]{1,0:T(2,128)S(1)} %constant_dynamic-update-slice_fusion, f32[6,768]{1,0:T(8,128)S(1)} %stack.108, f32[3072]{0:T(1024)S(1)} %dynamic_update_slice.24), channel_id=1, replica_groups=mesh['dp'=16,'tensor'=2] {'dp','tensor'}, use_global_device_ids=true, to_apply=%region_35.37 | all-reduce | flops 9216 | bytes 73728 | tf_op jit(solution)/shard_map/psum | solution.py:291
  1170.4 8.1 reshape.370
  1186.6 28.2 %reduce-scatter.21.cloned.1.call-done = f32[48,1536]{1,0:T(8,128)} async-done(((f32[768,1536]{1,0:T(8,128)}), f32[48,1536]{1,0:T(8,128)}) %reduce-scatter.21.cloned.1.call-update) | async-done | bytes 294928 | tf_op jit(solution)/shard_map/reduce_scatter | solution.py:276
  1214.8 61.4 %reduce-scatter.19.cloned.1.call-done = f32[48,384]{1,0:T(8,128)} async-done(((f32[768,384]{1,0:T(8,128)}), f32[48,384]{1,0:T(8,128)}) %reduce-scatter.19.cloned.1.call-update) | async-done | bytes 73744 | tf_op jit(solution)/shard_map/reduce_scatter | solution.py:275
  1276.2 71.6 %reduce-scatter.17.cloned.1.call-done = f32[48,3,384]{2,0,1:T(8,128)} async-done(((f32[768,3,384]{2,0,1:T(8,128)}), f32[48,3,384]{2,0,1:T(8,128)}) %reduce-scatter.17.cloned.1.call-update) | async-done | bytes 221200 | tf_op jit(solution)/shard_map/reduce_scatter | solution.py:274
  (575 shorter events, 550.0 us)
Async XLA Ops:
  7.2 126.4 %all-gather.8.cloned.1.call-start = ((), (), s32[]{:S(2)}) async-start(), calls=%async_computation.11 | async-start | bytes 4718592 | tf_op jit(solution)/shard_map/all_gather | solution.py:166
  10.7 71.8 %collective-permute-start.14 = (bf16[1,1,64,768]{3,2,0,1:T(8,128)(2,1)S(1)}, bf16[1,1,64,768]{3,2,0,1:T(8,128)(2,1)S(1)}, u32[]{:S(2)}, u32[]{:S(2)}) collective-permute-start(bf16[1,1,64,768]{3,2,0,1:T(8,128)(2,1)S(1)} %constant_dynamic-slice_fusion.2), channel_id=1, source_target_pairs={{0,30},{2,0},{4,2},{6,4},{8,6},{10,8},{12,10},{14,12},{16,14},{18,... | collective-permute-start | bytes 294920 | tf_op jit(solution)/shard_map/ppermute | solution.py:27
  16.6 65.8 %collective-permute-start.13 = (bf16[1,1,64,768]{3,2,1,0:T(8,128)(2,1)S(1)}, bf16[1,1,64,768]{3,2,1,0:T(8,128)(2,1)S(1)}, u32[]{:S(2)}, u32[]{:S(2)}) collective-permute-start(bf16[1,1,64,768]{3,2,1,0:T(8,128)(2,1)S(1)} %get-tuple-element.269), channel_id=1, source_target_pairs={{0,28},{2,30},{4,0},{6,2},{8,4},{10,6},{12,8},{14,10},{16,12},{18,... | collective-permute-start | bytes 294920 | tf_op jit(solution)/shard_map/ppermute | solution.py:27
  17.4 65.0 %collective-permute-start.12 = (bf16[1,1,64,768]{3,2,1,0:T(8,128)(2,1)S(1)}, bf16[1,1,64,768]{3,2,1,0:T(8,128)(2,1)S(1)}, u32[]{:S(2)}, u32[]{:S(2)}) collective-permute-start(bf16[1,1,64,768]{3,2,1,0:T(8,128)(2,1)S(1)} %get-tuple-element.270), channel_id=1, source_target_pairs={{0,26},{2,28},{4,30},{6,0},{8,2},{10,4},{12,6},{14,8},{16,10},{18,... | collective-permute-start | bytes 294920 | tf_op jit(solution)/shard_map/ppermute | solution.py:27
  17.5 64.8 %collective-permute-start.11 = (bf16[1,1,64,768]{3,2,1,0:T(8,128)(2,1)S(1)}, bf16[1,1,64,768]{3,2,1,0:T(8,128)(2,1)S(1)}, u32[]{:S(2)}, u32[]{:S(2)}) collective-permute-start(bf16[1,1,64,768]{3,2,1,0:T(8,128)(2,1)S(1)} %get-tuple-element.271), channel_id=1, source_target_pairs={{0,24},{2,26},{4,28},{6,30},{8,0},{10,2},{12,4},{14,6},{16,8},{18,... | collective-permute-start | bytes 294920 | tf_op jit(solution)/shard_map/ppermute | solution.py:27
  17.9 6.9 collective-permute-start
  24.8 7.3 collective-permute-start.1
  32.2 5.8 collective-permute-start.2
  38.0 6.4 collective-permute-start.3
  44.4 5.8 collective-permute-start.4
  50.3 6.4 collective-permute-start.5
  56.7 5.6 collective-permute-start.6
  62.3 5.5 collective-permute-start.7
  67.8 4.9 collective-permute-start.8
  72.8 5.5 collective-permute-start.9
  78.3 4.0 collective-permute-start.10
  84.3 92.7 %all-gather.10.cloned.1.call-start = ((), (), s32[]{:S(2)}) async-start(), calls=%async_computation.12 | async-start | bytes 1880064 | tf_op jit(solution)/shard_map/all_gather | solution.py:154
  85.0 292.8 %reduce-scatter.9.cloned.1.call-start = ((), (), s32[]{:S(2)}) async-start(), calls=%async_computation.13 | async-start | bytes 4718592 | tf_op jit(solution)/shard_map/reduce_scatter | solution.py:180
  335.6 87.3 %all-gather.14.cloned.1.call-start = ((), (), s32[]{:S(2)}) async-start(), calls=%async_computation.15 | async-start | bytes 2506752 | tf_op jit(solution)/shard_map/all_gather | solution.py:156
  337.2 131.3 %all-gather.12.cloned.1.call-start = ((), (), s32[]{:S(2)}) async-start(), calls=%async_computation.14 | async-start | bytes 4718592 | tf_op jit(solution)/shard_map/all_gather | solution.py:191
  383.0 130.6 %all-gather.16.cloned.1.call-start = ((), (), s32[]{:S(2)}) async-start(), calls=%async_computation.16 | async-start | bytes 2506752 | tf_op jit(solution)/shard_map/all_gather | solution.py:157
  383.7 186.1 %reduce-scatter.11.cloned.1.call-start = ((), (), s32[]{:S(2)}) async-start(), calls=%async_computation.17 | async-start | bytes 4718592 | tf_op jit(solution)/shard_map/reduce_scatter | solution.py:194
  522.7 102.1 %all-gather.18.cloned.1.call-start = ((), (), s32[]{:S(2)}) async-start(), calls=%async_computation.18 | async-start | bytes 4718592 | tf_op jit(solution)/shard_map/all_gather | solution.py:215
  579.3 110.6 %reduce-scatter.13.cloned.1.call-start = ((), (), s32[]{:S(2)}) async-start(), calls=%async_computation.19 | async-start | bytes 4718592 | tf_op jit(solution)/shard_map/reduce_scatter | solution.py:222
  646.2 98.7 %all-gather.20.cloned.1.call-start = ((), (), s32[]{:S(2)}) async-start(), calls=%async_computation.20 | async-start | bytes 4718592 | tf_op jit(solution)/shard_map/all_gather | solution.py:234
  699.8 351.2 %reduce-scatter.15.cloned.1.call-start = ((), (), s32[]{:S(2)}) async-start(), calls=%async_computation.21 | async-start | bytes 4718592 | tf_op jit(solution)/shard_map/reduce_scatter | solution.py:265
  986.9 199.7 %reduce-scatter.23.cloned.1.call-start = ((), (), s32[]{:S(2)}) async-start(), calls=%async_computation.25 | async-start | bytes 5013504 | tf_op jit(solution)/shard_map/reduce_scatter | solution.py:277
  998.4 216.5 %reduce-scatter.21.cloned.1.call-start = ((), (), s32[]{:S(2)}) async-start(), calls=%async_computation.24 | async-start | bytes 5013504 | tf_op jit(solution)/shard_map/reduce_scatter | solution.py:276
  1009.7 266.5 %reduce-scatter.19.cloned.1.call-start = ((), (), s32[]{:S(2)}) async-start(), calls=%async_computation.23 | async-start | bytes 1253376 | tf_op jit(solution)/shard_map/reduce_scatter | solution.py:275
  1036.5 46.1 %all-to-all-start = ((bf16[16,2,24576]{2,1,0:T(2,128)(2,1)}), bf16[16,2,24576]{2,1,0:T(2,128)(2,1)}, u32[]{:S(2)}, u32[]{:S(2)}) async-start(bf16[16,2,24576]{2,1,0:T(2,128)(2,1)} %reshape.367), calls=%async_computation.2 | async-start | bytes 3145728 | tf_op jit(solution)/shard_map/all_to_all | solution.py:295
  1042.2 305.6 %reduce-scatter.17.cloned.1.call-start = ((), (), s32[]{:S(2)}) async-start(), calls=%async_computation.22 | async-start | bytes 3760128 | tf_op jit(solution)/shard_map/reduce_scatter | solution.py:274
  1082.6 87.7 %all-to-all-start.2 = ((bf16[16,2,24576]{2,1,0:T(2,128)(2,1)}), bf16[16,2,24576]{2,1,0:T(2,128)(2,1)}, u32[]{:S(2)}, u32[]{:S(2)}) async-start(bf16[16,2,24576]{2,1,0:T(2,128)(2,1)} %reshape.369), calls=%async_computation.6 | async-start | bytes 3145728 | tf_op jit(solution)/shard_map/all_to_all | solution.py:298
  (75 other events, 910.8 us)
Sparse Core Ops, SparseCore 0:
  84.4 49.1 all-gather.7
  136.5 40.4 all-gather.9
  335.7 42.1 reduce-scatter.8
  380.6 42.2 all-gather.13
  424.9 43.6 all-gather.11
  471.2 42.2 all-gather.15
  522.8 42.1 reduce-scatter.10
  579.4 45.2 all-gather.17
  646.4 43.4 reduce-scatter.12
  700.0 44.8 all-gather.19
  987.0 43.4 reduce-scatter.14
  1034.8 94.6 reduce-scatter.22
  1134.0 80.8 reduce-scatter.20
  1218.9 57.2 reduce-scatter.18
  1280.5 67.2 reduce-scatter.16
